TPU v7x, 32 devices: a whole 2x2x4 slice. The times are simulated.
32 devices in a mesh: tm: 4 (over z), map: 8 (over y, x, core).
Axes of the slice: x: 2, y: 2, z: 4, core: 2. Of those that a mesh axis runs over, the one named last changes fastest.
Arguments:
- points: float32 [3, 32768, 128], P(None, ('tm', 'map')), may hold values from -6 to 6
- poses: float32 [6, 1024], P(None, ('tm', 'map')), may hold values from -1.5 to 1.5
- normal_angles: float32 [2, 8192], P(None, ('tm', 'map')), may hold values from -3.140625 to 3.140625
- voxel_ids: int32 [32768], P(('tm', 'map')), may hold values from -1 to 8191, as said below
- scan_ids: int32 [32768], P(('tm', 'map')), may hold values from 0 to 255
Outputs:
- hessian: float32 [36, 1024], P(None, ('tm', 'map'))
- gradient: float32 [6, 1024], P(None, ('tm', 'map'))
- plane_cost: float32 [8192], P(('tm', 'map'))
Inputs may be any that keep to these rules, and one draw needn't show every extreme that they name: `voxel_ids`: -1 marks an empty slot. Otherwise the block at position s among the 1024 blocks of its device has its voxel among those of owner o = s // 32, that is, in [o * 256, (o + 1) * 256), where owners are devices in tm+map order. In every draw some owner gets a live block in every slot from every device.
All inputs are finite; a program needn't handle non-finite values.
Results may differ from a plain program's by a relative error of at most 0.0003.
Values sent between devices are 32-bit elements; how exact they have to be, the bound alone decides.
A program may use at most 128 MiB of HBM per device.

v0:
```python
import jax
import jax.numpy as jnp
from jax import lax
from jax.sharding import PartitionSpec as P


def rigid(angles):
    cos_x, sin_x = (jnp.cos(angles[0]), jnp.sin(angles[0]))
    cos_y, sin_y = (jnp.cos(angles[1]), jnp.sin(angles[1]))
    cos_z, sin_z = (jnp.cos(angles[2]), jnp.sin(angles[2]))
    return jnp.stack(
        [
            cos_z * cos_y,
            cos_z * sin_y * sin_x - sin_z * cos_x,
            cos_z * sin_y * cos_x + sin_z * sin_x,
            sin_z * cos_y,
            sin_z * sin_y * sin_x + cos_z * cos_x,
            sin_z * sin_y * cos_x - cos_z * sin_x,
            -sin_y,
            cos_y * sin_x,
            cos_y * cos_x,
            angles[3],
            angles[4],
            angles[5],
        ]
    )


def transform(points, per_block):
    rows_out = []
    for axis_out in range(3):
        acc = per_block[9 + axis_out][:, None]
        for axis_in in range(3):
            acc = acc + per_block[3 * axis_out + axis_in][:, None] * points[axis_in]
        rows_out.append(acc)
    return jnp.stack(rows_out)


def moments_of(world_pts):
    first = jnp.sum(world_pts, axis=2)
    pairs = [(0, 0), (1, 1), (2, 2), (0, 1), (0, 2), (1, 2)]
    second = jnp.stack([jnp.sum(world_pts[i] * world_pts[j], axis=1) for i, j in pairs])
    return jnp.concatenate([first, second], axis=0)


def unit_normal(normal_angles):
    theta, phi = (normal_angles[0], normal_angles[1])
    return jnp.stack([jnp.sin(theta) * jnp.cos(phi), jnp.sin(theta) * jnp.sin(phi), jnp.cos(theta)])


def moment_terms(moments, normal, offset, weight):
    zeros = jnp.zeros_like(normal[0])
    skew = jnp.stack(
        [
            jnp.stack([zeros, normal[2], -normal[1]]),
            jnp.stack([-normal[2], zeros, normal[0]]),
            jnp.stack([normal[1], -normal[0], zeros]),
        ]
    )
    second = jnp.stack(
        [
            jnp.stack([moments[3], moments[6], moments[7]]),
            jnp.stack([moments[6], moments[4], moments[8]]),
            jnp.stack([moments[7], moments[8], moments[5]]),
        ]
    )
    first = moments[:3]
    skew_second = jnp.einsum("ikb,kjb->ijb", skew, second, precision=lax.Precision.HIGHEST)
    upper_left = jnp.einsum("ikb,jkb->ijb", skew_second, skew, precision=lax.Precision.HIGHEST)
    skew_first = jnp.einsum("ikb,kb->ib", skew, first, precision=lax.Precision.HIGHEST)
    upper_right = skew_first[:, None, :] * normal[None, :, :]
    lower_right = weight[None, None, :] * normal[:, None, :] * normal[None, :, :]
    top = jnp.concatenate([upper_left, upper_right], axis=1)
    bottom = jnp.concatenate([jnp.transpose(upper_right, (1, 0, 2)), lower_right], axis=1)
    outer = jnp.concatenate([top, bottom], axis=0).reshape(36, -1)
    grad_top = (
        jnp.einsum("ijb,jb->ib", skew_second, normal, precision=lax.Precision.HIGHEST)
        - offset[None, :] * skew_first
    )
    grad_low = normal * (jnp.sum(normal * first, axis=0) - weight * offset)[None, :]
    return jnp.concatenate([outer, grad_top, grad_low], axis=0)


def local(points, poses, normal_angles, voxel_ids, scan_ids):
    blocks = points.shape[1]
    npoints = points.shape[2]
    devices = lax.axis_size(("tm", "map"))
    slots = blocks // devices
    vox_count = normal_angles.shape[1]
    pose_row = lax.all_gather(poses, "map", axis=1, tiled=True)
    pose_table = rigid(pose_row)
    scan_count = pose_row.shape[1]
    per_block = jnp.take(pose_table, scan_ids, axis=1)
    world_pts = transform(points, per_block)
    is_live = voxel_ids >= 0
    owner_of = jnp.arange(blocks, dtype=jnp.int32) // slots
    local_ids = jnp.where(is_live, voxel_ids - owner_of * vox_count, -1)
    own_moments = jnp.where(is_live[None, :], moments_of(world_pts), 0.0)
    sent = own_moments.reshape(9, devices, slots)
    labels = local_ids.reshape(1, devices, slots)
    recv_moments, recv_labels = (
        lax.all_to_all(sent, ("tm", "map"), split_axis=1, concat_axis=1, tiled=True),
        lax.all_to_all(labels, ("tm", "map"), split_axis=1, concat_axis=1, tiled=True),
    )
    moments = recv_moments.reshape(9, blocks)
    flat_ids = recv_labels[0].reshape(blocks)
    vox_hot = (flat_ids[None, :] == jnp.arange(vox_count, dtype=jnp.int32)[:, None]).astype(
        jnp.float32
    )
    voxel_sums = lax.dot_general(
        moments, vox_hot, (((1,), (1,)), ((), ())), precision=lax.Precision.HIGHEST
    )
    counts = jnp.sum(vox_hot, axis=1) * npoints
    floor_count = jnp.maximum(counts, 1.0)
    normal = unit_normal(normal_angles)
    offset = jnp.sum(normal * voxel_sums[:3], axis=0) / floor_count
    quadric = (
        normal[0] ** 2 * voxel_sums[3]
        + normal[1] ** 2 * voxel_sums[4]
        + normal[2] ** 2 * voxel_sums[5]
        + 2.0
        * (
            normal[0] * normal[1] * voxel_sums[6]
            + normal[0] * normal[2] * voxel_sums[7]
            + normal[1] * normal[2] * voxel_sums[8]
        )
    )
    plane_cost = quadric / floor_count - offset**2
    reply = jnp.dot(
        jnp.concatenate([normal, offset[None, :]], axis=0), vox_hot, precision=lax.Precision.HIGHEST
    )
    all_scans = poses.shape[1] * devices
    scale = all_scans / (blocks * devices * npoints)
    returned = lax.all_to_all(
        reply.reshape(4, devices, slots), ("tm", "map"), split_axis=1, concat_axis=1, tiled=True
    ).reshape(4, blocks)
    own_weight = is_live.astype(jnp.float32) * npoints
    terms = moment_terms(own_moments, returned[:3], returned[3], own_weight)
    per_scan = jax.ops.segment_sum(terms.T, scan_ids, num_segments=scan_count).T * scale
    shares = lax.psum_scatter(per_scan, "map", scatter_dimension=1, tiled=True)
    return (shares[:36], shares[36:], plane_cost)


def solution(mesh):
    return jax.shard_map(
        local,
        mesh=mesh,
        in_specs=(
            P(None, ("tm", "map"), None),
            P(None, ("tm", "map")),
            P(None, ("tm", "map")),
            P(("tm", "map")),
            P(("tm", "map")),
        ),
        out_specs=(P(None, ("tm", "map")), P(None, ("tm", "map")), P(("tm", "map"))),
        check_vma=False,
    )
```

profile of v0, /device:TPU:0, one launch (start us, length us, event | category | flops | bytes accessed | tf_op | source)
XLA Modules:
  0.0 143.4 jit_solution(6349652086940309007)
XLA Ops:
  7.2 0.7 broadcast_select_fusion.2
  7.9 0.7 fusion.22
  8.6 0.7 reshape.235
  9.2 7.3 %all-to-all-start.1 = ((s32[1,32,32]{2,0,1:T(1,128)}), s32[1,32,32]{2,0,1:T(1,128)S(1)}, u32[]{:S(2)}, u32[]{:S(2)}) async-start(s32[1,32,32]{2,0,1:T(1,128)} %reshape.235), calls=%async_computation.1 | async-start | bytes 32768 | tf_op jit(solution)/shard_map/all_to_all | solution.py:103
  16.6 9.5 %all-gather = f32[8,32,6]{1,2,0:T(8,128)S(1)} all-gather(f32[1,32,6]{1,2,0:T(8,128)} %bitcast.134), channel_id=1, replica_groups=mesh['tm'=4,'map'=8] {'map'}, dimensions={0}, use_global_device_ids=true | all-gather | bytes 6912 | tf_op jit(solution)/shard_map/all_gather | solution.py:90
  26.1 0.1 reshape.264
  26.2 0.1 fusion.42
  26.3 0.1 multiply_subtract_fusion.3
  26.4 0.7 fusion.34
  27.1 0.7 compare_and_fusion
  27.8 0.1 copy.139
  27.9 2.8 %gather_fusion = f32[1024,12]{1,0:T(8,128)S(1)} fusion(f32[12,256]{0,1:T(8,128)S(1)} %copy.139, s32[1024]{0:T(1024)S(1)} %fusion.34), kind=kCustom, calls=%fused_computation | custom fusion | bytes 102400 | tf_op jit(solution)/shard_map/jit(_take)/gather | solution.py:93
  30.8 0.2 select_bitcast_fusion
  31.0 3.2 %slice_reduce_fusion.11 = (f32[1024]{0:T(1024)S(1)}, f32[1024]{0:T(1024)S(1)}, f32[1024]{0:T(1024)S(1)}, f32[1024]{0:T(1024)S(1)}, f32[1024]{0:T(1024)S(1)}, /*i...) fusion(f32[12,1024]{0,1:T(8,128)S(1)} %select_bitcast_fusion), kind=kLoop, calls=%fused_computation.22 | loop fusion | bytes 98304 | tf_op jit(solution)/shard_map/slice | solution.py:32
  34.2 1.3 multiply_add_fusion.2
  35.5 2.2 %fusion.7 = (f32[1024,128]{1,0:T(8,128)S(1)}, f32[1024,128]{1,0:T(8,128)}) fusion(f32[3,1024,128]{2,1,0:T(8,128)S(1)} %copy-done, f32[1024]{0:T(1024)S(1)} %get-tuple-element.39, f32[1024]{0:T(1024)S(1)} %get-tuple-element.40, f32[1024]{0:T(1024)S(1)} %get-tuple-element.41, f32[1024]{0:T(1024)S(1)} %get-tuple-element.30, f32[1024]{0:T(1024)S(1)} %get-tuple-element.31, ...), kind=kLoop, calls=%fused_computation.26 | loop fusion | flops 1572864 | bytes 2654208 | tf_op jit(solution)/shard_map/add | solution.py:34
  37.7 0.1 broadcast_in_dim.49
  37.8 0.8 multiply_add_fusion.1
  38.6 0.5 maximum_reduce_fusion
  39.1 0.1 concatenate.36
  39.2 2.6 %multiply_reduce_fusion.1 = (f32[1024]{0:T(1024)S(1)}, f32[1024]{0:T(1024)S(1)}, f32[1024]{0:T(1024)S(1)}, f32[1024]{0:T(1024)S(1)}, f32[1024]{0:T(1024)S(1)}, /*index=5*/f32[1024]{0:T(1024)S(1)}) fusion(f32[1024,128]{1,0:T(8,128)} %get-tuple-element.54, f32[1024,128]{1,0:T(8,128)S(1)} %get-tuple-element.53, f32[3,1024,128]{2,1,0:T(8,128)S(1)} %copy-done, ...), kind=kLoop, calls=%fused_computation.44 | loop fusion | flops 2353152 | bytes 2662400 | tf_op jit(solution)/shard_map/reduce_sum | solution.py:42
  41.9 0.1 concatenate.37
  42.5 0.2 concatenate.43
  42.7 0.7 reshape.314
  43.5 4.5 %all-to-all-start = ((f32[32,1,288]{2,1,0:T(1,128)}), f32[32,1,288]{2,1,0:T(1,128)S(1)}, u32[]{:S(2)}, u32[]{:S(2)}) async-start(f32[32,1,288]{2,1,0:T(1,128)} %reshape.314), calls=%async_computation | async-start | bytes 98304 | tf_op jit(solution)/shard_map/all_to_all | solution.py:102
  48.0 0.5 broadcast.146
  48.5 0.7 reduce.47
  49.2 0.1 eq.15
  49.3 0.2 convert_reduce_fusion
  49.5 5.9 %all-to-all-done = f32[32,1,288]{2,1,0:T(1,128)S(1)} async-done(((f32[32,1,288]{2,1,0:T(1,128)}), f32[32,1,288]{2,1,0:T(1,128)S(1)}, u32[]{:S(2)}, u32[]{:S(2)}) %all-to-all-start) | async-done | bytes 36896 | tf_op jit(solution)/shard_map/all_to_all | solution.py:102
  55.3 0.5 broadcast.147
  55.8 0.8 reduce.48
  56.6 0.1 reshape.315
  56.8 0.1 reshape.234
  56.9 0.6 fusion.6
  57.5 0.1 fusion.38
  57.6 0.6 multiply_subtract_fusion.1
  58.2 0.4 fusion.5
  58.6 0.1 reshape.236
  58.7 0.7 reshape.316
  59.5 2.5 %all-to-all-start.2 = ((f32[32,1,128]{2,1,0:T(1,128)}), f32[32,1,128]{2,1,0:T(1,128)S(1)}, u32[]{:S(2)}, u32[]{:S(2)}) async-start(f32[32,1,128]{2,1,0:T(1,128)} %reshape.316), calls=%async_computation.2 | async-start | bytes 32768 | tf_op jit(solution)/shard_map/all_to_all | solution.py:134
  62.0 0.2 reduce-scatter.2.cloned.1.call-start
  62.3 1.8 %copy.149 = f32[3,3,1024]{0,1,2:T(4,128)} copy(f32[3,3,1024]{2,1,0:T(4,128)S(1)} %pad_maximum_fusion.1) | data formatting | bytes 73728 | tf_op jit(solution)/shard_map/stack | solution.py:60
  64.0 5.1 %all-to-all-done.2 = f32[32,1,128]{2,1,0:T(1,128)S(1)} async-done(((f32[32,1,128]{2,1,0:T(1,128)}), f32[32,1,128]{2,1,0:T(1,128)S(1)}, u32[]{:S(2)}, u32[]{:S(2)}) %all-to-all-start.2) | async-done | bytes 16416 | tf_op jit(solution)/shard_map/all_to_all | solution.py:134
  69.1 0.7 reduce.49
  69.8 0.1 reshape.317
  69.9 0.2 slice_reduce_fusion.15
  70.1 0.1 mul.428
  70.2 0.1 mul.440
  70.3 0.2 copy.171
  70.6 0.1 squeeze.11
  70.6 0.1 slice.219
  70.7 0.1 slice.222
  70.9 0.9 copy.151
  71.8 13.2 %multiply_reduce_fusion = (f32[1024,3]{1,0:T(8,128)S(1)}, f32[1024,3,3]{2,1,0:T(4,128)}) fusion(f32[1024,3]{1,0:T(8,128)S(1)} %copy.171, f32[3,3,1024]{0,1,2:T(4,128)} %copy.149, f32[3,3,1024]{1,0,2:T(4,128)S(1)} %copy.151), kind=kOutput, calls=%fused_computation.4 | convolution fusion | flops 347136 | bytes 135168 | tf_op jit(solution)/shard_map/ikb,kjb->ijb/dot_general | solution.py:68
  85.0 0.2 copy.169
  85.2 10.7 %fusion.2 = f32[3,3,1024]{1,0,2:T(4,128)} fusion(f32[3,3,1024]{1,0,2:T(4,128)S(1)} %copy.151, f32[1024,3,3]{2,1,0:T(4,128)} %get-tuple-element.83), kind=kOutput, calls=%fused_computation.5 | convolution fusion | flops 331776 | bytes 110592 | tf_op jit(solution)/shard_map/ikb,jkb->ijb/dot_general | solution.py:69
  95.9 1.8 %copy.154 = f32[3,3,1024]{2,1,0:T(4,128)S(1)} copy(f32[3,3,1024]{1,0,2:T(4,128)} %fusion.2) | data formatting | bytes 73728 | tf_op jit(solution)/shard_map/ikb,jkb->ijb/transpose | solution.py:69
  97.9 0.2 copy.155
  98.1 6.2 %scatter_custom_fusion = f32[256,42]{1,0:T(8,128)S(1)} fusion(s32[1024]{0:T(1024)} %param.9, f32[1024,42]{1,0:T(8,128)S(1)} %copy.155, f32[]{:T(128)} %constant.17.clone.1), kind=kCustom, calls=%fused_computation.57 | custom fusion | flops 43008 | bytes 43520 | tf_op jit(solution)/shard_map/scatter-add | solution.py:139
  104.3 0.6 multiply_bitcast_fusion
  105.0 30.1 %reduce-scatter.2.cloned.1.call-done = f32[42,32]{0,1:T(8,128)} async-done(((f32[42,256]{0,1:T(8,128)}), f32[42,32]{0,1:T(8,128)}) %reduce-scatter.2.cloned.1.call-update) | async-done | bytes 5392 | tf_op jit(solution)/shard_map/reduce_scatter | solution.py:140
  135.1 0.8 slice.274
  135.9 0.7 copy.156
  (42 shorter events, 1.1 us)
Async XLA Ops:
  9.2 34.2 %all-to-all-start.1 = ((s32[1,32,32]{2,0,1:T(1,128)}), s32[1,32,32]{2,0,1:T(1,128)S(1)}, u32[]{:S(2)}, u32[]{:S(2)}) async-start(s32[1,32,32]{2,0,1:T(1,128)} %reshape.235), calls=%async_computation.1 | async-start | bytes 32768 | tf_op jit(solution)/shard_map/all_to_all | solution.py:103
  31.0 3.2 %copy-start = (f32[3,1024,128]{2,1,0:T(8,128)S(1)}, f32[3,1024,128]{2,1,0:T(8,128)}, u32[]{:S(2)}) copy-start(f32[3,1024,128]{2,1,0:T(8,128)} %param.5) | copy-start | bytes 4718596
  41.9 15.6 %copy-start.1 = (f32[2,256]{1,0:T(2,128)S(1)}, f32[2,256]{1,0:T(2,128)}, u32[]{:S(2)}) copy-start(f32[2,256]{1,0:T(2,128)} %param.7) | copy-start | bytes 6148
  43.5 11.8 %all-to-all-start = ((f32[32,1,288]{2,1,0:T(1,128)}), f32[32,1,288]{2,1,0:T(1,128)S(1)}, u32[]{:S(2)}, u32[]{:S(2)}) async-start(f32[32,1,288]{2,1,0:T(1,128)} %reshape.314), calls=%async_computation | async-start | bytes 98304 | tf_op jit(solution)/shard_map/all_to_all | solution.py:102
  59.5 9.7 %all-to-all-start.2 = ((f32[32,1,128]{2,1,0:T(1,128)}), f32[32,1,128]{2,1,0:T(1,128)S(1)}, u32[]{:S(2)}, u32[]{:S(2)}) async-start(f32[32,1,128]{2,1,0:T(1,128)} %reshape.316), calls=%async_computation.2 | async-start | bytes 32768 | tf_op jit(solution)/shard_map/all_to_all | solution.py:134
  62.0 73.1 %reduce-scatter.2.cloned.1.call-start = ((), (), s32[]{:S(2)}) async-start(), calls=%async_computation.4 | async-start | bytes 147456 | tf_op jit(solution)/shard_map/reduce_scatter | solution.py:140
Sparse Core Ops, SparseCore 0:
  105.1 29.9 reduce-scatter.1
where the time goes:
time: 144 us; the launch traced here: 143 us
  waiting for transfers between devices  41.1 us (29%)
  matrix products  24.9 us (17%)
  other arithmetic  20.9 us (15%)
  local copies, waits for them, and re-layouts  18 us (12%)
  starting transfers between devices  14.6 us (10%)
  between operations  14.4 us (10%)
  blocking collectives  9.49 us (7%)
    reduce_scatter x1, waiting for transfers between devices, local(): shares = lax.psum_scatter(per_scan, 'map', scatter_dimension=1, tiled=True)  30.1 us
    dot_general x1, matrix products, moment_terms(): jnp.einsum('ikb,kjb->ijb', skew, second, precision=lax.Precision.HIGHEST)  13.2 us
    dot_general x1, matrix products, moment_terms(): jnp.einsum('ikb,jkb->ijb', skew_second, skew, precision=lax.Precision.HIG...  10.7 us
    all_gather x1, blocking collectives, local(): pose_row = lax.all_gather(poses, 'map', axis=1, tiled=True)  9.49 us
    all_to_all x1, starting transfers between devices, local(): lax.all_to_all(labels, ('tm', 'map'), split_axis=1, concat_axis=1, tiled=...  7.33 us
    scatter-add x1, other arithmetic, local(): jax.ops.segment_sum(terms.T, scan_ids, num_segments=scan_count).T * scale  6.18 us
    all_to_all x1, waiting for transfers between devices, local(): lax.all_to_all(sent, ('tm', 'map'), split_axis=1, concat_axis=1, tiled=True)  5.86 us
    all_to_all x1, waiting for transfers between devices, local(): lax.all_to_all(reply.reshape(4, devices, slots), ('tm', 'map'), split_axi...  5.1 us
  transfers between devices with their start and end apart: 4, of which 3 were waited for; matrix products, arithmetic and copies ran while one was open for 14% of the time, Pallas kernels for 0%

commit v1 on v0

v1 whole, which is shorter than its diff:
```python
import functools

import jax
import jax.numpy as jnp
from jax import lax
from jax.experimental import pallas as pl
from jax.experimental.pallas import tpu as pltpu
from jax.sharding import PartitionSpec as P

LANES = 128
MESH = pl.DeviceIdType.MESH
PAIRS = [(0, 0), (1, 1), (2, 2), (0, 1), (0, 2), (1, 2)]
PAIR_ROW = {}
for _k, (_i, _j) in enumerate(PAIRS):
    PAIR_ROW[(_i, _j)] = _k
    PAIR_ROW[(_j, _i)] = _k


def parts_of(x):
    high = x.astype(jnp.bfloat16)
    rest = x - high.astype(jnp.float32)
    mid = rest.astype(jnp.bfloat16)
    low = (rest - mid.astype(jnp.float32)).astype(jnp.bfloat16)
    return jnp.concatenate([high, mid, low], axis=0)


def joined(y):
    rows = y.shape[0] // 3
    return y[:rows] + y[rows : 2 * rows] + y[2 * rows :]


def group_turn(pieces, out_group, group, lanes_per):
    total = None
    for a, piece in enumerate(pieces):
        shift = lax.rem((a - out_group) * lanes_per + LANES, LANES)
        if isinstance(out_group, int):
            shift = ((a - out_group) * lanes_per) % LANES
        moved = piece if isinstance(shift, int) and shift == 0 else pltpu.roll(piece, shift, 1)
        total = moved if total is None else jnp.where(group == a, moved, total)
    return total


def loop(count, body):
    if count <= 8:
        for i in range(count):
            body(i)
    else:
        def step(i, carry):
            body(i)
            return carry

        lax.fori_loop(0, count, step, 0)


def kernel(
    sizes,
    points,
    poses,
    angles,
    voxel_ids,
    scan_ids,
    hess_out,
    grad_out,
    cost_out,
    pts,
    pose_pad,
    send0,
    recv0,
    raw,
    table,
    world,
    vox_row,
    send1,
    recv1,
    moved,
    send2,
    recv2,
    back,
    terms,
    send3,
    recv3,
    pts_sem,
    sends,
    recvs,
):
    n_tm, n_map, slots, npoints, scale = sizes
    devices = n_tm * n_map
    blocks = pts.shape[1]
    chunks = blocks // LANES
    per = LANES // slots
    own_scans = poses.shape[1]
    spread = LANES // own_scans
    scans = own_scans * n_map
    wide = scans // LANES
    voxels = angles.shape[1]
    tm = lax.axis_index("tm")
    mp = lax.axis_index("map")
    me = tm * n_map + mp

    def place(q):
        return (q // n_map, lax.rem(q, n_map))

    def chunk_copy(r):
        rows = pl.ds(r * LANES, LANES)
        return pltpu.make_async_copy(points.at[:, rows, :], pts.at[:, rows, :], pts_sem.at[r])

    loop(chunks, lambda r: chunk_copy(r).start())
    barrier = pltpu.get_barrier_semaphore()

    def greet(i, carry):
        pl.semaphore_signal(
            barrier, inc=1, device_id=place(lax.rem(me + i, devices)), device_id_type=MESH
        )
        return carry

    lax.fori_loop(1, devices, greet, 0)

    lane = lax.broadcasted_iota(jnp.int32, (8, LANES), 1)

    pose_pad[...] = jnp.zeros_like(pose_pad)
    pose_pad[0:6, 0:own_scans] = poses[...]
    mine = lax.rem(mp, spread)
    pose = pltpu.roll(pose_pad[...], mine * own_scans, 1)
    here = (lane // own_scans)[0:1] == mine
    cos, sin = jnp.cos(pose), jnp.sin(pose)
    cx, cy, cz = cos[0:1], cos[1:2], cos[2:3]
    sx, sy, sz = sin[0:1], sin[1:2], sin[2:3]
    rows = [
        cz * cy,
        cz * sy * sx - sz * cx,
        cz * sy * cx + sz * sx,
        sz * cy,
        sz * sy * sx + cz * cx,
        sz * sy * cx - cz * sx,
        -sy,
        cy * sx,
        cy * cx,
        pose[3:4],
        pose[4:5],
        pose[5:6],
    ]
    send0[...] = jnp.zeros_like(send0)
    for k, row in enumerate(rows):
        send0[k : k + 1, :] = jnp.where(here, row, 0.0)
    recv0[mp] = send0[...]

    theta, phi = angles[0:1, :], angles[1:2, :]
    sin_theta = jnp.sin(theta)
    normal = [sin_theta * jnp.cos(phi), sin_theta * jnp.sin(phi), jnp.cos(theta)]

    def raw_moments(r):
        chunk_copy(r).wait()
        at = pl.ds(r * LANES, LANES)
        xyz = [pts[i, at, :].T for i in range(3)]
        sums = [jnp.sum(x, axis=0, keepdims=True) for x in xyz]
        sums += [jnp.sum(xyz[i] * xyz[j], axis=0, keepdims=True) for i, j in PAIRS]
        for k, row in enumerate(sums):
            raw[pl.ds(r * 16 + k, 1), :] = row

    half = chunks // 2
    loop(half, raw_moments)
    pl.semaphore_wait(barrier, devices - 1)

    def map_copy(i, source, dest, s):
        peer = lax.rem(mp + i, n_map)
        return pltpu.make_async_remote_copy(
            src_ref=source(peer),
            dst_ref=dest.at[mp],
            send_sem=sends.at[s],
            recv_sem=recvs.at[s],
            device_id=(tm, peer),
            device_id_type=MESH,
        )

    for i in range(1, n_map):
        map_copy(i, lambda peer: send0, recv0, 0).start()
    loop(chunks - half, lambda r: raw_moments(half + r))

    def wait_bytes(ref, sem):
        pltpu.make_async_copy(ref, ref, sem).wait()

    wait_bytes(recv0.at[pl.ds(0, n_map - 1)], recvs.at[0])

    halves = []
    for h in range(wide):
        total = recv0[h * spread]
        for a in range(1, spread):
            total = total + recv0[h * spread + a]
        halves.append(total)
    pose_parts = parts_of(jnp.concatenate(halves, axis=1))

    scan_iota = lax.broadcasted_iota(jnp.int32, (scans, LANES), 0)

    def scan_hot(r):
        return jnp.where(scan_ids[pl.ds(r, 1), :] == scan_iota, 1.0, 0.0).astype(jnp.bfloat16)

    def look_up(r):
        found = jnp.dot(pose_parts, scan_hot(r), preferred_element_type=jnp.float32)
        table[pl.ds(pl.multiple_of(r * 16, 16), 16), :] = joined(found)

    loop(chunks, look_up)

    def every(ref, k, stride):
        return ref[pl.ds(k, chunks, stride=stride), :]

    first = [every(raw, k, 16) for k in range(3)]
    second = [every(raw, 3 + k, 16) for k in range(6)]
    rot = [[every(table, 3 * i + j, 16) for j in range(3)] for i in range(3)]
    shift = [every(table, 9 + i, 16) for i in range(3)]
    turned = [sum(rot[i][j] * first[j] for j in range(3)) for i in range(3)]
    half_turned = [
        [sum(rot[i][k] * second[PAIR_ROW[(k, j)]] for k in range(3)) for j in range(3)]
        for i in range(3)
    ]
    m1 = [turned[i] + npoints * shift[i] for i in range(3)]
    m2 = [
        sum(half_turned[i][k] * rot[j][k] for k in range(3))
        + turned[i] * shift[j]
        + shift[i] * m1[j]
        for i, j in PAIRS
    ]
    ids = voxel_ids[...]
    row_of = lax.broadcasted_iota(jnp.int32, ids.shape, 0)
    lane_of = lax.broadcasted_iota(jnp.int32, ids.shape, 1)
    owner_of = row_of * per + lane_of // slots
    local_ids = jnp.where(ids >= 0, ids - owner_of * voxels, -1).astype(jnp.float32)
    world[...] = jnp.zeros_like(world)
    for k, value in enumerate(m1 + m2 + [local_ids]):
        world[pl.ds(8 * (k // 4) + k % 4, chunks, stride=24), :] = value

    group = lane // slots

    def pack(r):
        pieces = [world[pl.ds(pl.multiple_of(r * 24 + 8 * c, 8), 8), :] for c in range(3)]
        for g in range(per):
            send1[r * per + g] = group_turn(pieces, g, group, slots)[0:4]

    loop(chunks, pack)

    def all_copy(i, source, dest, s):
        peer = lax.rem(me + i, devices)
        return pltpu.make_async_remote_copy(
            src_ref=source(peer),
            dst_ref=dest.at[me],
            send_sem=sends.at[s],
            recv_sem=recvs.at[s],
            device_id=place(peer),
            device_id_type=MESH,
        )

    def send_all(source, dest, s):
        def step(i, carry):
            all_copy(i, source, dest, s).start()
            return carry

        lax.fori_loop(1, devices, step, 0)

    send_all(lambda peer: send1.at[peer], recv1, 1)
    recv1[me] = send1[me]
    wait_bytes(recv1.at[pl.ds(0, devices - 1)], recvs.at[1])

    vox_iota = lax.broadcasted_iota(jnp.int32, (voxels, LANES), 0).astype(jnp.float32)
    zero4 = jnp.zeros((4, LANES), jnp.float32)

    def unpack(r):
        pieces = [jnp.concatenate([recv1[r * per + g], zero4], axis=0) for g in range(per)]
        for c in range(3):
            moved[pl.ds(pl.multiple_of(r * 24 + 8 * c, 8), 8), :] = group_turn(
                pieces, c, group, slots
            )

    loop(chunks, unpack)

    def vox_hot(r):
        row = moved[pl.ds(r * 24 + 17, 1), :]
        return jnp.where(row == vox_iota, 1.0, 0.0).astype(jnp.bfloat16)

    contract_last = (((1,), (1,)), ((), ()))
    row_id = lax.broadcasted_iota(jnp.int32, (24, LANES), 0)

    def add_voxels(r, acc):
        values = moved[pl.ds(pl.multiple_of(r * 24, 8), 24), :]
        values = jnp.where(row_id == 17, 1.0, values)
        return acc + lax.dot_general(
            parts_of(values), vox_hot(r), contract_last, preferred_element_type=jnp.float32
        )

    def summed(body, rows, columns):
        acc = jnp.zeros((rows, columns), jnp.float32)
        if chunks <= 8:
            for r in range(chunks):
                acc = body(r, acc)
            return acc
        return lax.fori_loop(0, chunks, body, acc)

    sums = joined(summed(add_voxels, 72, voxels))
    s1 = [sums[0:1], sums[1:2], sums[2:3]]
    s2 = [sums[3:4], sums[8:9], sums[9:10], sums[10:11], sums[11:12], sums[16:17]]
    floor_count = jnp.maximum(sums[17:18] * npoints, 1.0)
    offset = sum(normal[i] * s1[i] for i in range(3)) / floor_count
    quadric = sum(normal[i] ** 2 * s2[i] for i in range(3)) + 2.0 * sum(
        normal[PAIRS[k][0]] * normal[PAIRS[k][1]] * s2[k] for k in range(3, 6)
    )
    cost_out[...] = quadric / floor_count - offset**2
    vox_row[...] = jnp.zeros_like(vox_row)
    for k, row in enumerate(normal + [offset]):
        vox_row[k : k + 1, :] = row
    reply_parts = parts_of(vox_row[...])

    def reply(r):
        found = jnp.dot(reply_parts, vox_hot(r), preferred_element_type=jnp.float32)
        send2[r] = joined(found)[0:4]

    loop(chunks, reply)
    send_all(lambda peer: send2.at[peer // per], recv2, 2)
    recv2[me] = send2[me // per]
    wait_bytes(recv2.at[pl.ds(0, devices - 1)], recvs.at[2])

    my_group = lax.rem(me, per)

    def unpack_reply(r):
        pieces = [jnp.concatenate([recv2[r * per + g], zero4], axis=0) for g in range(per)]
        back[pl.ds(pl.multiple_of(r * 8, 8), 8), :] = group_turn(pieces, my_group, group, slots)

    loop(chunks, unpack_reply)
    n = [every(back, c, 8) for c in range(3)]
    d = every(back, 3, 8)

    def skew(v):
        return [n[2] * v[1] - n[1] * v[2], n[0] * v[2] - n[2] * v[0], n[1] * v[0] - n[0] * v[1]]

    full = [[m2[PAIR_ROW[(i, j)]] for j in range(3)] for i in range(3)]
    columns = [skew([full[k][j] for k in range(3)]) for j in range(3)]
    left = [[columns[j][i] for j in range(3)] for i in range(3)]
    upper = [skew(left[i]) for i in range(3)]
    skew_first = skew(m1)
    found = {}
    for i in range(3):
        for j in range(3):
            if j >= i:
                found[("h", i, j)] = upper[i][j]
                found[("h", 3 + i, 3 + j)] = npoints * n[i] * n[j]
            found[("h", i, 3 + j)] = skew_first[i] * n[j]
    rest = n[0] * m1[0] + n[1] * m1[1] + n[2] * m1[2] - npoints * d
    for i in range(3):
        found[("g", i)] = sum(left[i][j] * n[j] for j in range(3)) - d * skew_first[i]
        found[("g", 3 + i)] = n[i] * rest
    row_for = {}
    for k, (name, value) in enumerate(found.items()):
        row_for[name] = k
        terms[pl.ds(k, chunks, stride=32), :] = value
    for k in range(len(found), 32):
        terms[pl.ds(k, chunks, stride=32), :] = jnp.zeros_like(d)

    def add_scans(r, acc):
        values = parts_of(terms[pl.ds(pl.multiple_of(r * 32, 32), 32), :])
        return acc + lax.dot_general(
            values, scan_hot(r), contract_last, preferred_element_type=jnp.float32
        )

    per_scan = joined(summed(add_scans, 96, scans)) * scale
    scan_group = lane // own_scans
    for h in range(wide):
        pieces = [
            per_scan[8 * c : 8 * c + 8, h * LANES : (h + 1) * LANES] for c in range(4)
        ]
        for b in range(spread):
            send3[h * spread + b] = group_turn(pieces, b, scan_group, own_scans)
    for i in range(1, n_map):
        map_copy(i, lambda peer: send3.at[peer], recv3, 3).start()
    recv3[mp] = send3[mp]
    wait_bytes(recv3.at[pl.ds(0, n_map - 1)], recvs.at[3])
    total = recv3[0]
    for m in range(1, n_map):
        total = total + recv3[m]
    lined = [total] + [pltpu.roll(total, LANES - own_scans * c, 1) for c in range(1, 4)]

    def row_at(k):
        return lined[k // 8][k % 8 : k % 8 + 1, 0:own_scans]

    for i in range(6):
        for j in range(6):
            hess_out[6 * i + j : 6 * i + j + 1, :] = row_at(
                row_for[("h", min(i, j), max(i, j))]
            )
        grad_out[i : i + 1, :] = row_at(row_for[("g", i)])

    wait_bytes(recv0.at[pl.ds(0, n_map - 1)], sends.at[0])
    wait_bytes(send1.at[pl.ds(0, devices - 1)], sends.at[1])
    wait_bytes(recv2.at[pl.ds(0, devices - 1)], sends.at[2])
    wait_bytes(send3.at[pl.ds(0, n_map - 1)], sends.at[3])


def local(points, poses, normal_angles, voxel_ids, scan_ids):
    blocks, npoints = points.shape[1:]
    n_tm, n_map = lax.axis_size("tm"), lax.axis_size("map")
    devices = n_tm * n_map
    slots = blocks // devices
    chunks = blocks // LANES
    vox_count = normal_angles.shape[1]
    own_scans = poses.shape[1]
    assert LANES % slots == 0 and own_scans * 4 == LANES and n_map % 4 == 0
    assert npoints == LANES and slots * 4 == LANES
    scale = own_scans * devices / (blocks * devices * npoints)
    f32 = jnp.float32
    vmem = pl.BlockSpec(memory_space=pltpu.VMEM)
    hess, grad, cost = pl.pallas_call(
        functools.partial(kernel, (n_tm, n_map, slots, float(npoints), scale)),
        out_shape=(
            jax.ShapeDtypeStruct((36, own_scans), f32),
            jax.ShapeDtypeStruct((6, own_scans), f32),
            jax.ShapeDtypeStruct((1, vox_count), f32),
        ),
        in_specs=[pl.BlockSpec(memory_space=pl.ANY)] + [vmem] * 4,
        out_specs=(vmem, vmem, vmem),
        scratch_shapes=[
            pltpu.VMEM(points.shape, f32),
            pltpu.VMEM((8, LANES), f32),
            pltpu.VMEM((16, LANES), f32),
            pltpu.VMEM((n_map, 16, LANES), f32),
            pltpu.VMEM((chunks * 16, LANES), f32),
            pltpu.VMEM((chunks * 16, LANES), f32),
            pltpu.VMEM((chunks * 24, LANES), f32),
            pltpu.VMEM((8, vox_count), f32),
            pltpu.VMEM((devices, 4, LANES), f32),
            pltpu.VMEM((devices, 4, LANES), f32),
            pltpu.VMEM((chunks * 24, LANES), f32),
            pltpu.VMEM((chunks, 4, LANES), f32),
            pltpu.VMEM((devices, 4, LANES), f32),
            pltpu.VMEM((chunks * 8, LANES), f32),
            pltpu.VMEM((chunks * 32, LANES), f32),
            pltpu.VMEM((n_map, 8, LANES), f32),
            pltpu.VMEM((n_map, 8, LANES), f32),
            pltpu.SemaphoreType.DMA((chunks,)),
            pltpu.SemaphoreType.DMA((4,)),
            pltpu.SemaphoreType.DMA((4,)),
        ],
        compiler_params=pltpu.CompilerParams(collective_id=0, has_side_effects=True),
    )(
        points,
        poses,
        normal_angles,
        voxel_ids.reshape(chunks, LANES),
        scan_ids.reshape(chunks, LANES),
    )
    return hess, grad, cost.reshape(vox_count)


def solution(mesh):
    return jax.shard_map(
        local,
        mesh=mesh,
        in_specs=(
            P(None, ("tm", "map"), None),
            P(None, ("tm", "map")),
            P(None, ("tm", "map")),
            P(("tm", "map")),
            P(("tm", "map")),
        ),
        out_specs=(P(None, ("tm", "map")), P(None, ("tm", "map")), P(("tm", "map"))),
        check_vma=False,
    )
```

time: 144 us -> 30.8 us (0.21)
  waiting for transfers between devices: 41.1 us -> 0 us
  Pallas kernels: 0 us -> 26 us
  matrix products: 24.9 us -> 0 us
  other arithmetic: 20.9 us -> 0 us
  starting transfers between devices: 14.6 us -> 0 us
  local copies, waits for them, and re-layouts: 18 us -> 3.88 us
  between operations: 14.4 us -> 0.64 us
  blocking collectives: 9.49 us -> 0 us
    reduce_scatter x1 -> x0, waiting for transfers between devices: 30.1 us -> none  [local(): shares = lax.psum_scatter(per_scan, 'map', scatter_dimension=1, tiled=True)]
    pallas_call x0 -> x1, Pallas kernels: none -> 26 us  [local(): pl.pallas_call(functools.partial(kernel, (n_tm, n_map, slots, float(npoin...]
    dot_general x4 -> x0, matrix products: 24.9 us -> none  [the longest x1 13.2 us: moment_terms(): jnp.einsum('ikb,kjb->ijb', skew, second, precision=lax.Precision.HIGHEST)]
    all_to_all x3 -> x0, starting transfers between devices: 14.4 us -> none  [the longest x1 7.33 us: local(): lax.all_to_all(labels, ('tm', 'map'), split_axis=1, concat_axis=1, tiled=...]
    all_to_all x3 -> x0, waiting for transfers between devices: 11 us -> none  [the longest x1 5.86 us: local(): lax.all_to_all(sent, ('tm', 'map'), split_axis=1, concat_axis=1, tiled=True)]
    all_gather x1 -> x0, blocking collectives: 9.49 us -> none  [local(): pose_row = lax.all_gather(poses, 'map', axis=1, tiled=True)]
    scatter-add x1 -> x0, other arithmetic: 6.18 us -> none  [local(): jax.ops.segment_sum(terms.T, scan_ids, num_segments=scan_count).T * scale]
    add x4 -> x0, other arithmetic: 4.45 us -> none  [the longest x3 4.36 us: transform(): acc = acc + per_block[3 * axis_out + axis_in][:, None] * points[axis_in]]
  transfers between devices with their start and end apart: 4 -> 0, of which waited for: 3 -> 0; matrix products, arithmetic and copies ran while one was open for 14% -> 0% of each run, Pallas kernels for 0% -> 0%
where the time goes in v1:
time: 30.8 us; the launch traced here: 30.5 us
  Pallas kernels  26 us (84%)
  local copies, waits for them, and re-layouts  3.88 us (13%)
  between operations  0.64 us (2%)
    pallas_call x1, Pallas kernels, local(): pl.pallas_call(functools.partial(kernel, (n_tm, n_map, slots, float(npoin...  26 us
    unnamed x3, local copies, waits for them, and re-layouts  3.88 us

profile of v1, /device:TPU:0, one launch (start us, length us, event | category | flops | bytes accessed | tf_op | source)
XLA Modules:
  0.0 30.5 jit_solution(6118422864924991039)
XLA Ops:
  0.6 26.0 %shard_map.76 = (f32[36,32]{1,0:T(8,128)}, f32[6,32]{1,0:T(8,128)}, f32[1,256]{1,0:T(1,128)}) custom-call(f32[3,1024,128]{2,1,0:T(8,128)} %points.1, f32[6,32]{1,0:T(8,128)} %poses.1, f32[2,256]{1,0:T(2,128)} %angles.1, s32[8,128]{1,0:T(8,128)} %bitcast.3, s32[8,128]{1,0:T(8,128)} %bitcast.4), custom_call_target="tpu_custom_call" | custom-call | tf_op jit(solution)/shard_map/pallas_call | solution.py:407
  26.6 1.4 %copy.8 = f32[36,32]{0,1:T(8,128)} copy(f32[36,32]{1,0:T(8,128)} %get-tuple-element.9) | data formatting | bytes 9216
  28.1 1.3 %copy.11 = f32[6,32]{1,0:T(8,128)} copy(f32[6,32]{1,0:T(8,128)} %get-tuple-element.16) | data formatting | bytes 1536
  29.3 1.2 %copy.12 = f32[256]{0:T(256)} copy(f32[256]{0:T(256)} %bitcast.5) | data formatting | bytes 2048

commit v2 on v1

--- a/solution.py
+++ b/solution.py
@@ -14,6 +14,9 @@
 for _k, (_i, _j) in enumerate(PAIRS):
     PAIR_ROW[(_i, _j)] = _k
     PAIR_ROW[(_j, _i)] = _k
+
+
+ROWS = [("h", i, j) for i in range(6) for j in range(i, 6)] + [("g", i) for i in range(6)]
 
 
 def parts_of(x):
@@ -59,9 +62,7 @@
     angles,
     voxel_ids,
     scan_ids,
-    hess_out,
-    grad_out,
-    cost_out,
+    packed,
     pts,
     pose_pad,
     send0,
@@ -237,8 +238,12 @@
 
     loop(chunks, pack)
 
+    upper = tm // (n_tm // 2)
+
     def all_copy(i, source, dest, s):
-        peer = lax.rem(me + i, devices)
+        step = lax.rem(i, devices) // n_map
+        tm_peer = (1 - upper) * (n_tm - 1 - step) + upper * step
+        peer = tm_peer * n_map + lax.rem(mp + i, n_map)
         return pltpu.make_async_remote_copy(
             src_ref=source(peer),
             dst_ref=dest.at[me],
@@ -246,14 +251,19 @@
             recv_sem=recvs.at[s],
             device_id=place(peer),
             device_id_type=MESH,
-        )
+        ), peer
 
     def send_all(source, dest, s):
-        def step(i, carry):
-            all_copy(i, source, dest, s).start()
+        def start_with(i, carry):
+            copy, peer = all_copy(i, source, dest, s)
+
+            @pl.when(peer != me)
+            def _():
+                copy.start()
+
             return carry
 
-        lax.fori_loop(1, devices, step, 0)
+        lax.fori_loop(0, devices, start_with, 0, unroll=4)
 
     send_all(lambda peer: send1.at[peer], recv1, 1)
     recv1[me] = send1[me]
@@ -301,7 +311,9 @@
     quadric = sum(normal[i] ** 2 * s2[i] for i in range(3)) + 2.0 * sum(
         normal[PAIRS[k][0]] * normal[PAIRS[k][1]] * s2[k] for k in range(3, 6)
     )
-    cost_out[...] = quadric / floor_count - offset**2
+    cost = quadric / floor_count - offset**2
+    for h in range(voxels // LANES):
+        packed[8 + h : 9 + h, :] = cost[:, h * LANES : (h + 1) * LANES]
     vox_row[...] = jnp.zeros_like(vox_row)
     for k, row in enumerate(normal + [offset]):
         vox_row[k : k + 1, :] = row
@@ -309,22 +321,25 @@
 
     def reply(r):
         found = jnp.dot(reply_parts, vox_hot(r), preferred_element_type=jnp.float32)
-        send2[r] = joined(found)[0:4]
-
+        value = joined(found)
+        rolled = [value] + [pltpu.roll(value, slots * a, 1) for a in range(1, per)]
+        for g in range(per):
+            total = jnp.zeros_like(value)
+            for c in range(4):
+                total = jnp.where(corner & (group == c), rolled[(c - g) % per], total)
+            send2[r * per + g] = jnp.sum(total, axis=0, keepdims=True)
+
+    corner = lax.broadcasted_iota(jnp.int32, (8, LANES), 0) == group
     loop(chunks, reply)
-    send_all(lambda peer: send2.at[peer // per], recv2, 2)
-    recv2[me] = send2[me // per]
+    send_all(lambda peer: send2.at[peer], recv2, 2)
+    recv2[me] = send2[me]
     wait_bytes(recv2.at[pl.ds(0, devices - 1)], recvs.at[2])
 
-    my_group = lax.rem(me, per)
-
-    def unpack_reply(r):
-        pieces = [jnp.concatenate([recv2[r * per + g], zero4], axis=0) for g in range(per)]
-        back[pl.ds(pl.multiple_of(r * 8, 8), 8), :] = group_turn(pieces, my_group, group, slots)
-
-    loop(chunks, unpack_reply)
-    n = [every(back, c, 8) for c in range(3)]
-    d = every(back, 3, 8)
+    back[...] = recv2[...].reshape(devices, LANES)
+    pieces = [back[pl.ds(g, chunks, stride=per), :] for g in range(per)]
+    wide_group = lane_of // slots
+    n = [group_turn(pieces, c, wide_group, slots) for c in range(3)]
+    d = group_turn(pieces, 3, wide_group, slots)
 
     def skew(v):
         return [n[2] * v[1] - n[1] * v[2], n[0] * v[2] - n[2] * v[0], n[1] * v[0] - n[0] * v[1]]
@@ -332,22 +347,21 @@
     full = [[m2[PAIR_ROW[(i, j)]] for j in range(3)] for i in range(3)]
     columns = [skew([full[k][j] for k in range(3)]) for j in range(3)]
     left = [[columns[j][i] for j in range(3)] for i in range(3)]
-    upper = [skew(left[i]) for i in range(3)]
+    corner_block = [skew(left[i]) for i in range(3)]
     skew_first = skew(m1)
     found = {}
     for i in range(3):
         for j in range(3):
             if j >= i:
-                found[("h", i, j)] = upper[i][j]
+                found[("h", i, j)] = corner_block[i][j]
                 found[("h", 3 + i, 3 + j)] = npoints * n[i] * n[j]
             found[("h", i, 3 + j)] = skew_first[i] * n[j]
     rest = n[0] * m1[0] + n[1] * m1[1] + n[2] * m1[2] - npoints * d
     for i in range(3):
         found[("g", i)] = sum(left[i][j] * n[j] for j in range(3)) - d * skew_first[i]
         found[("g", 3 + i)] = n[i] * rest
-    row_for = {}
-    for k, (name, value) in enumerate(found.items()):
-        row_for[name] = k
+    for name, value in found.items():
+        k = ROWS.index(name)
         terms[pl.ds(k, chunks, stride=32), :] = value
     for k in range(len(found), 32):
         terms[pl.ds(k, chunks, stride=32), :] = jnp.zeros_like(d)
@@ -373,22 +387,31 @@
     total = recv3[0]
     for m in range(1, n_map):
         total = total + recv3[m]
-    lined = [total] + [pltpu.roll(total, LANES - own_scans * c, 1) for c in range(1, 4)]
-
-    def row_at(k):
-        return lined[k // 8][k % 8 : k % 8 + 1, 0:own_scans]
-
-    for i in range(6):
-        for j in range(6):
-            hess_out[6 * i + j : 6 * i + j + 1, :] = row_at(
-                row_for[("h", min(i, j), max(i, j))]
-            )
-        grad_out[i : i + 1, :] = row_at(row_for[("g", i)])
+    packed[0:8, :] = total
 
     wait_bytes(recv0.at[pl.ds(0, n_map - 1)], sends.at[0])
     wait_bytes(send1.at[pl.ds(0, devices - 1)], sends.at[1])
     wait_bytes(recv2.at[pl.ds(0, devices - 1)], sends.at[2])
     wait_bytes(send3.at[pl.ds(0, n_map - 1)], sends.at[3])
+
+
+def finish(packed, hess_out, grad_out, cost_out, lines):
+    own_scans = grad_out.shape[1]
+    total = packed[0:8, :]
+    lined = [total] + [pltpu.roll(total, LANES - own_scans * c, 1) for c in range(1, 4)]
+
+    def row_at(name):
+        k = ROWS.index(name)
+        return lined[k // 8][k % 8 : k % 8 + 1]
+
+    lines[...] = jnp.zeros_like(lines)
+    for i in range(6):
+        for j in range(6):
+            lines[6 * i + j : 6 * i + j + 1, :] = row_at(("h", min(i, j), max(i, j)))
+        grad_out[i : i + 1, :] = row_at(("g", i))[:, 0:own_scans]
+    hess_out[...] = lines[...].T[0:own_scans, 0:36]
+    for h in range(cost_out.shape[1] // LANES):
+        cost_out[:, h * LANES : (h + 1) * LANES] = packed[8 + h : 9 + h, :]
 
 
 def local(points, poses, normal_angles, voxel_ids, scan_ids):
@@ -404,15 +427,12 @@
     scale = own_scans * devices / (blocks * devices * npoints)
     f32 = jnp.float32
     vmem = pl.BlockSpec(memory_space=pltpu.VMEM)
-    hess, grad, cost = pl.pallas_call(
+    extra = -(-(vox_count // LANES) // 8) * 8
+    packed = pl.pallas_call(
         functools.partial(kernel, (n_tm, n_map, slots, float(npoints), scale)),
-        out_shape=(
-            jax.ShapeDtypeStruct((36, own_scans), f32),
-            jax.ShapeDtypeStruct((6, own_scans), f32),
-            jax.ShapeDtypeStruct((1, vox_count), f32),
-        ),
+        out_shape=jax.ShapeDtypeStruct((8 + extra, LANES), f32),
         in_specs=[pl.BlockSpec(memory_space=pl.ANY)] + [vmem] * 4,
-        out_specs=(vmem, vmem, vmem),
+        out_specs=vmem,
         scratch_shapes=[
             pltpu.VMEM(points.shape, f32),
             pltpu.VMEM((8, LANES), f32),
@@ -425,9 +445,9 @@
             pltpu.VMEM((devices, 4, LANES), f32),
             pltpu.VMEM((devices, 4, LANES), f32),
             pltpu.VMEM((chunks * 24, LANES), f32),
-            pltpu.VMEM((chunks, 4, LANES), f32),
-            pltpu.VMEM((devices, 4, LANES), f32),
-            pltpu.VMEM((chunks * 8, LANES), f32),
+            pltpu.VMEM((devices, 1, LANES), f32),
+            pltpu.VMEM((devices, 1, LANES), f32),
+            pltpu.VMEM((devices, LANES), f32),
             pltpu.VMEM((chunks * 32, LANES), f32),
             pltpu.VMEM((n_map, 8, LANES), f32),
             pltpu.VMEM((n_map, 8, LANES), f32),
@@ -443,7 +463,18 @@
         voxel_ids.reshape(chunks, LANES),
         scan_ids.reshape(chunks, LANES),
     )
-    return hess, grad, cost.reshape(vox_count)
+    hess, grad, cost = pl.pallas_call(
+        finish,
+        out_shape=(
+            jax.ShapeDtypeStruct((own_scans, 36), f32),
+            jax.ShapeDtypeStruct((6, own_scans), f32),
+            jax.ShapeDtypeStruct((1, vox_count), f32),
+        ),
+        in_specs=[vmem],
+        out_specs=(vmem, vmem, vmem),
+        scratch_shapes=[pltpu.VMEM((LANES, LANES), f32)],
+    )(packed)
+    return hess.T, grad, cost.reshape(vox_count)
 
 
 def solution(mesh):

time: 30.8 us -> 27.9 us (0.906)
  local copies, waits for them, and re-layouts: 3.88 us -> 0 us
  Pallas kernels: 26 us -> 27 us
    unnamed x3 -> x0, local copies, waits for them, and re-layouts: 3.88 us -> none
    pallas_call x0 -> x1, Pallas kernels: none -> 1.45 us  [local(): pl.pallas_call(finish, out_shape=(jax.ShapeDtypeStruct((own_scans, 36), f...]
    pallas_call x1, Pallas kernels: 26 us -> 25.5 us  [local(): pl.pallas_call(functools.partial(kernel, (n_tm, n_map, slots, float(npoin...]
where the time goes in v2:
time: 27.9 us; the launch traced here: 27.6 us
  Pallas kernels  27 us (97%)
  between operations  0.64 us (2%)
    pallas_call x1, Pallas kernels, local(): pl.pallas_call(functools.partial(kernel, (n_tm, n_map, slots, float(npoin...  25.5 us
    pallas_call x1, Pallas kernels, local(): pl.pallas_call(finish, out_shape=(jax.ShapeDtypeStruct((own_scans, 36), f...  1.45 us

profile of v2, /device:TPU:0, one launch (start us, length us, event | category | flops | bytes accessed | tf_op | source)
XLA Modules:
  0.0 27.6 jit_solution(5454212820506491663)
XLA Ops:
  0.6 25.5 %shard_map.76.packed = f32[16,128]{1,0:T(8,128)} custom-call(f32[3,1024,128]{2,1,0:T(8,128)} %points.1, f32[6,32]{1,0:T(8,128)} %poses.1, f32[2,256]{1,0:T(2,128)} %angles.1, s32[8,128]{1,0:T(8,128)} %bitcast.4, s32[8,128]{1,0:T(8,128)} %bitcast.5), custom_call_target="tpu_custom_call" | custom-call | tf_op jit(solution)/shard_map/pallas_call | solution.py:431
  26.1 1.5 %shard_map.77 = (f32[32,36]{1,0:T(8,128)}, f32[6,32]{1,0:T(8,128)}, f32[1,256]{1,0:T(1,128)}) custom-call(f32[16,128]{1,0:T(8,128)} %shard_map.76.packed), custom_call_target="tpu_custom_call" | custom-call | tf_op jit(solution)/shard_map/pallas_call | solution.py:466

commit v3 on v2

--- a/solution.py
+++ b/solution.py
@@ -65,10 +65,8 @@
     packed,
     pts,
     pose_pad,
-    send0,
-    recv0,
-    raw,
     table,
+    sent,
     world,
     vox_row,
     send1,
@@ -119,10 +117,9 @@
     lane = lax.broadcasted_iota(jnp.int32, (8, LANES), 1)
 
     pose_pad[...] = jnp.zeros_like(pose_pad)
-    pose_pad[0:6, 0:own_scans] = poses[...]
-    mine = lax.rem(mp, spread)
-    pose = pltpu.roll(pose_pad[...], mine * own_scans, 1)
-    here = (lane // own_scans)[0:1] == mine
+    for g in range(spread):
+        pose_pad[0:6, g * own_scans : (g + 1) * own_scans] = poses[...]
+    pose = pose_pad[...]
     cos, sin = jnp.cos(pose), jnp.sin(pose)
     cx, cy, cz = cos[0:1], cos[1:2], cos[2:3]
     sx, sy, sz = sin[0:1], sin[1:2], sin[2:3]
@@ -140,10 +137,22 @@
         pose[4:5],
         pose[5:6],
     ]
-    send0[...] = jnp.zeros_like(send0)
+    sent[...] = jnp.zeros_like(sent)
+
+    def sent_row(k):
+        return 8 * (k // 6) + k % 6
+
     for k, row in enumerate(rows):
-        send0[k : k + 1, :] = jnp.where(here, row, 0.0)
-    recv0[mp] = send0[...]
+        sent[pl.ds(sent_row(11 + k), chunks, stride=32), :] = jnp.broadcast_to(
+            row, (chunks, LANES)
+        )
+    ids = voxel_ids[...]
+    row_of = lax.broadcasted_iota(jnp.int32, ids.shape, 0)
+    lane_of = lax.broadcasted_iota(jnp.int32, ids.shape, 1)
+    owner_of = row_of * per + lane_of // slots
+    local_ids = jnp.where(ids >= 0, ids - owner_of * voxels, -1).astype(jnp.float32)
+    sent[pl.ds(sent_row(9), chunks, stride=32), :] = local_ids
+    sent[pl.ds(sent_row(10), chunks, stride=32), :] = scan_ids[...].astype(jnp.float32)
 
     theta, phi = angles[0:1, :], angles[1:2, :]
     sin_theta = jnp.sin(theta)
@@ -156,10 +165,17 @@
         sums = [jnp.sum(x, axis=0, keepdims=True) for x in xyz]
         sums += [jnp.sum(xyz[i] * xyz[j], axis=0, keepdims=True) for i, j in PAIRS]
         for k, row in enumerate(sums):
-            raw[pl.ds(r * 16 + k, 1), :] = row
-
-    half = chunks // 2
-    loop(half, raw_moments)
+            sent[pl.ds(r * 32 + sent_row(k), 1), :] = row
+
+    group = lane // slots
+
+    def pack(r):
+        raw_moments(r)
+        pieces = [sent[pl.ds(pl.multiple_of(r * 32 + 8 * c, 8), 8), :] for c in range(4)]
+        for g in range(per):
+            send1[r * per + g] = group_turn(pieces, g, group, slots)[0:6]
+
+    loop(chunks, pack)
     pl.semaphore_wait(barrier, devices - 1)
 
     def map_copy(i, source, dest, s):
@@ -173,70 +189,36 @@
             device_id_type=MESH,
         )
 
-    for i in range(1, n_map):
-        map_copy(i, lambda peer: send0, recv0, 0).start()
-    loop(chunks - half, lambda r: raw_moments(half + r))
-
     def wait_bytes(ref, sem):
         pltpu.make_async_copy(ref, ref, sem).wait()
 
-    wait_bytes(recv0.at[pl.ds(0, n_map - 1)], recvs.at[0])
-
-    halves = []
-    for h in range(wide):
-        total = recv0[h * spread]
-        for a in range(1, spread):
-            total = total + recv0[h * spread + a]
-        halves.append(total)
-    pose_parts = parts_of(jnp.concatenate(halves, axis=1))
-
     scan_iota = lax.broadcasted_iota(jnp.int32, (scans, LANES), 0)
 
     def scan_hot(r):
         return jnp.where(scan_ids[pl.ds(r, 1), :] == scan_iota, 1.0, 0.0).astype(jnp.bfloat16)
 
-    def look_up(r):
-        found = jnp.dot(pose_parts, scan_hot(r), preferred_element_type=jnp.float32)
-        table[pl.ds(pl.multiple_of(r * 16, 16), 16), :] = joined(found)
-
-    loop(chunks, look_up)
-
     def every(ref, k, stride):
         return ref[pl.ds(k, chunks, stride=stride), :]
 
-    first = [every(raw, k, 16) for k in range(3)]
-    second = [every(raw, 3 + k, 16) for k in range(6)]
-    rot = [[every(table, 3 * i + j, 16) for j in range(3)] for i in range(3)]
-    shift = [every(table, 9 + i, 16) for i in range(3)]
-    turned = [sum(rot[i][j] * first[j] for j in range(3)) for i in range(3)]
-    half_turned = [
-        [sum(rot[i][k] * second[PAIR_ROW[(k, j)]] for k in range(3)) for j in range(3)]
-        for i in range(3)
-    ]
-    m1 = [turned[i] + npoints * shift[i] for i in range(3)]
-    m2 = [
-        sum(half_turned[i][k] * rot[j][k] for k in range(3))
-        + turned[i] * shift[j]
-        + shift[i] * m1[j]
-        for i, j in PAIRS
-    ]
-    ids = voxel_ids[...]
-    row_of = lax.broadcasted_iota(jnp.int32, ids.shape, 0)
-    lane_of = lax.broadcasted_iota(jnp.int32, ids.shape, 1)
-    owner_of = row_of * per + lane_of // slots
-    local_ids = jnp.where(ids >= 0, ids - owner_of * voxels, -1).astype(jnp.float32)
-    world[...] = jnp.zeros_like(world)
-    for k, value in enumerate(m1 + m2 + [local_ids]):
-        world[pl.ds(8 * (k // 4) + k % 4, chunks, stride=24), :] = value
-
-    group = lane // slots
-
-    def pack(r):
-        pieces = [world[pl.ds(pl.multiple_of(r * 24 + 8 * c, 8), 8), :] for c in range(3)]
-        for g in range(per):
-            send1[r * per + g] = group_turn(pieces, g, group, slots)[0:4]
-
-    loop(chunks, pack)
+    def transformed(source):
+        first = [every(source, sent_row(k), 32) for k in range(3)]
+        second = [every(source, sent_row(3 + k), 32) for k in range(6)]
+        pose_at = [every(table, sent_row(11 + k) - 8, 24) for k in range(12)]
+        rot = [pose_at[3 * i : 3 * i + 3] for i in range(3)]
+        shift = pose_at[9:]
+        turned = [sum(rot[i][j] * first[j] for j in range(3)) for i in range(3)]
+        half_turned = [
+            [sum(rot[i][k] * second[PAIR_ROW[(k, j)]] for k in range(3)) for j in range(3)]
+            for i in range(3)
+        ]
+        m1 = [turned[i] + npoints * shift[i] for i in range(3)]
+        m2 = [
+            sum(half_turned[i][k] * rot[j][k] for k in range(3))
+            + turned[i] * shift[j]
+            + shift[i] * m1[j]
+            for i, j in PAIRS
+        ]
+        return m1, m2
 
     upper = tm // (n_tm // 2)
 
@@ -270,27 +252,52 @@
     wait_bytes(recv1.at[pl.ds(0, devices - 1)], recvs.at[1])
 
     vox_iota = lax.broadcasted_iota(jnp.int32, (voxels, LANES), 0).astype(jnp.float32)
-    zero4 = jnp.zeros((4, LANES), jnp.float32)
+    zero2 = jnp.zeros((2, LANES), jnp.float32)
 
     def unpack(r):
-        pieces = [jnp.concatenate([recv1[r * per + g], zero4], axis=0) for g in range(per)]
-        for c in range(3):
-            moved[pl.ds(pl.multiple_of(r * 24 + 8 * c, 8), 8), :] = group_turn(
+        pieces = [jnp.concatenate([recv1[r * per + g], zero2], axis=0) for g in range(per)]
+        for c in range(4):
+            moved[pl.ds(pl.multiple_of(r * 32 + 8 * c, 8), 8), :] = group_turn(
                 pieces, c, group, slots
             )
 
     loop(chunks, unpack)
 
     def vox_hot(r):
-        row = moved[pl.ds(r * 24 + 17, 1), :]
+        row = moved[pl.ds(r * 32 + sent_row(9), 1), :]
         return jnp.where(row == vox_iota, 1.0, 0.0).astype(jnp.bfloat16)
 
+    float_iota = scan_iota.astype(jnp.float32)
+
+    def group_parts(t):
+        return parts_of(
+            jnp.concatenate(
+                [
+                    moved[pl.ds(pl.multiple_of((t * wide + h) * 32 + 8, 8), 24), :]
+                    for h in range(wide)
+                ],
+                axis=1,
+            )
+        )
+
+    def look_up(t):
+        table_parts = group_parts(t)
+        for h in range(wide):
+            r = t * wide + h
+            row = moved[pl.ds(r * 32 + sent_row(10), 1), :]
+            hot = jnp.where(row == float_iota, 1.0, 0.0).astype(jnp.bfloat16)
+            found = jnp.dot(table_parts, hot, preferred_element_type=jnp.float32)
+            table[pl.ds(pl.multiple_of(r * 24, 8), 24), :] = joined(found)
+
+    loop(n_tm, look_up)
+    m1, m2 = transformed(moved)
+    world[...] = jnp.ones_like(world)
+    for k, value in enumerate(m1 + m2):
+        world[pl.ds(k, chunks, stride=16), :] = value
+
     contract_last = (((1,), (1,)), ((), ()))
-    row_id = lax.broadcasted_iota(jnp.int32, (24, LANES), 0)
-
     def add_voxels(r, acc):
-        values = moved[pl.ds(pl.multiple_of(r * 24, 8), 24), :]
-        values = jnp.where(row_id == 17, 1.0, values)
+        values = world[pl.ds(pl.multiple_of(r * 16, 16), 16), :]
         return acc + lax.dot_general(
             parts_of(values), vox_hot(r), contract_last, preferred_element_type=jnp.float32
         )
@@ -303,10 +310,10 @@
             return acc
         return lax.fori_loop(0, chunks, body, acc)
 
-    sums = joined(summed(add_voxels, 72, voxels))
-    s1 = [sums[0:1], sums[1:2], sums[2:3]]
-    s2 = [sums[3:4], sums[8:9], sums[9:10], sums[10:11], sums[11:12], sums[16:17]]
-    floor_count = jnp.maximum(sums[17:18] * npoints, 1.0)
+    sums = joined(summed(add_voxels, 48, voxels))
+    s1 = [sums[k : k + 1] for k in range(3)]
+    s2 = [sums[3 + k : 4 + k] for k in range(6)]
+    floor_count = jnp.maximum(sums[9:10] * npoints, 1.0)
     offset = sum(normal[i] * s1[i] for i in range(3)) / floor_count
     quadric = sum(normal[i] ** 2 * s2[i] for i in range(3)) + 2.0 * sum(
         normal[PAIRS[k][0]] * normal[PAIRS[k][1]] * s2[k] for k in range(3, 6)
@@ -333,6 +340,15 @@
     loop(chunks, reply)
     send_all(lambda peer: send2.at[peer], recv2, 2)
     recv2[me] = send2[me]
+
+    own_parts = group_parts(tm)
+
+    def look_up_own(r):
+        found = jnp.dot(own_parts, scan_hot(r), preferred_element_type=jnp.float32)
+        table[pl.ds(pl.multiple_of(r * 24, 8), 24), :] = joined(found)
+
+    loop(chunks, look_up_own)
+    m1, m2 = transformed(sent)
     wait_bytes(recv2.at[pl.ds(0, devices - 1)], recvs.at[2])
 
     back[...] = recv2[...].reshape(devices, LANES)
@@ -381,18 +397,17 @@
         for b in range(spread):
             send3[h * spread + b] = group_turn(pieces, b, scan_group, own_scans)
     for i in range(1, n_map):
-        map_copy(i, lambda peer: send3.at[peer], recv3, 3).start()
+        map_copy(i, lambda peer: send3.at[peer], recv3, 0).start()
     recv3[mp] = send3[mp]
-    wait_bytes(recv3.at[pl.ds(0, n_map - 1)], recvs.at[3])
+    wait_bytes(recv3.at[pl.ds(0, n_map - 1)], recvs.at[0])
     total = recv3[0]
     for m in range(1, n_map):
         total = total + recv3[m]
     packed[0:8, :] = total
 
-    wait_bytes(recv0.at[pl.ds(0, n_map - 1)], sends.at[0])
     wait_bytes(send1.at[pl.ds(0, devices - 1)], sends.at[1])
     wait_bytes(recv2.at[pl.ds(0, devices - 1)], sends.at[2])
-    wait_bytes(send3.at[pl.ds(0, n_map - 1)], sends.at[3])
+    wait_bytes(send3.at[pl.ds(0, n_map - 1)], sends.at[0])
 
 
 def finish(packed, hess_out, grad_out, cost_out, lines):
@@ -436,15 +451,13 @@
         scratch_shapes=[
             pltpu.VMEM(points.shape, f32),
             pltpu.VMEM((8, LANES), f32),
-            pltpu.VMEM((16, LANES), f32),
-            pltpu.VMEM((n_map, 16, LANES), f32),
+            pltpu.VMEM((chunks * 24, LANES), f32),
+            pltpu.VMEM((chunks * 32, LANES), f32),
             pltpu.VMEM((chunks * 16, LANES), f32),
-            pltpu.VMEM((chunks * 16, LANES), f32),
-            pltpu.VMEM((chunks * 24, LANES), f32),
             pltpu.VMEM((8, vox_count), f32),
-            pltpu.VMEM((devices, 4, LANES), f32),
-            pltpu.VMEM((devices, 4, LANES), f32),
-            pltpu.VMEM((chunks * 24, LANES), f32),
+            pltpu.VMEM((devices, 6, LANES), f32),
+            pltpu.VMEM((devices, 6, LANES), f32),
+            pltpu.VMEM((chunks * 32, LANES), f32),
             pltpu.VMEM((devices, 1, LANES), f32),
             pltpu.VMEM((devices, 1, LANES), f32),
             pltpu.VMEM((devices, LANES), f32),
@@ -452,8 +465,8 @@
             pltpu.VMEM((n_map, 8, LANES), f32),
             pltpu.VMEM((n_map, 8, LANES), f32),
             pltpu.SemaphoreType.DMA((chunks,)),
-            pltpu.SemaphoreType.DMA((4,)),
-            pltpu.SemaphoreType.DMA((4,)),
+            pltpu.SemaphoreType.DMA((3,)),
+            pltpu.SemaphoreType.DMA((3,)),
         ],
         compiler_params=pltpu.CompilerParams(collective_id=0, has_side_effects=True),
     )(

time: 27.9 us -> 23.9 us (0.86)
  Pallas kernels: 27 us -> 23 us
    pallas_call x1, Pallas kernels: 25.5 us -> 21.6 us  [local(): pl.pallas_call(functools.partial(kernel, (n_tm, n_map, slots, float(npoin...]
where the time goes in v3:
time: 23.9 us; the launch traced here: 23.7 us
  Pallas kernels  23 us (96%)
  between operations  0.64 us (3%)
    pallas_call x1, Pallas kernels, local(): pl.pallas_call(functools.partial(kernel, (n_tm, n_map, slots, float(npoin...  21.6 us
    pallas_call x1, Pallas kernels, local(): pl.pallas_call(finish, out_shape=(jax.ShapeDtypeStruct((own_scans, 36), f...  1.45 us

profile of v3, /device:TPU:0, one launch (start us, length us, event | category | flops | bytes accessed | tf_op | source)
XLA Modules:
  0.0 23.7 jit_solution(16928661098907082103)
XLA Ops:
  0.6 21.6 %shard_map.76.packed = f32[16,128]{1,0:T(8,128)} custom-call(f32[3,1024,128]{2,1,0:T(8,128)} %points.1, f32[6,32]{1,0:T(8,128)} %poses.1, f32[2,256]{1,0:T(2,128)} %angles.1, s32[8,128]{1,0:T(8,128)} %bitcast.4, s32[8,128]{1,0:T(8,128)} %bitcast.5), custom_call_target="tpu_custom_call" | custom-call | tf_op jit(solution)/shard_map/pallas_call | solution.py:446
  22.2 1.5 %shard_map.77 = (f32[32,36]{1,0:T(8,128)}, f32[6,32]{1,0:T(8,128)}, f32[1,256]{1,0:T(1,128)}) custom-call(f32[16,128]{1,0:T(8,128)} %shard_map.76.packed), custom_call_target="tpu_custom_call" | custom-call | tf_op jit(solution)/shard_map/pallas_call | solution.py:479
